TPU v7x, 128 devices: a whole 4x4x4 slice. The times are simulated.
128 devices in a mesh: rows: 16 (over z_hi, x, core), cols: 8 (over z_lo, y).
Axes of the slice: x: 4, y: 4, z: 4 (z_hi: 2, z_lo: 2; z = z_hi * 2 + z_lo), core: 2. Of those that a mesh axis runs over, the one named last changes fastest.
Arguments:
- surface_field: float32 [8192, 16384], P('rows', 'cols'), may hold values from -20 to 30
- land_words: int32 [8192, 512], P('rows', 'cols'), may hold values from -2147483648 to 2147483646
Outputs:
- level_one: float32 [4096, 8192], P('rows', 'cols')
- level_two: float32 [2048, 4096], P('rows', 'cols')
- level_three: float32 [1024, 2048], P('rows', 'cols')
- level_four: float32 [512, 1024], P('rows', 'cols')
- level_means: float32 [4], replicated
- level_maxima: float32 [4], replicated
All inputs are finite; a program needn't handle non-finite values.
Results may differ from a plain program's by a relative error of at most 0.0001.
Values sent between devices are 32-bit elements; how exact they have to be, the bound alone decides.
A program may use at most 128 MiB of HBM per device.

v0:
```python
import math

import jax
import jax.numpy as jnp
from jax import lax
from jax.experimental import pallas as pl
from jax.experimental.pallas import tpu as pltpu
from jax.sharding import PartitionSpec as P

MESH = pl.DeviceIdType.MESH
F32 = jnp.float32
BF16 = jnp.bfloat16
HALO = 16
PAD = 24
LANES = 128
ROW_CHUNK = 64
FLOOR = 0.05
EPS = 1e-06


def lane_iota(rows, dtype=jnp.int32):
    return lax.broadcasted_iota(dtype, (rows, LANES), 1)


def tap_weight(offset):
    inner = jnp.logical_or(offset == 1, offset == 2)
    outer = jnp.logical_or(offset == 0, offset == 3)
    return jnp.where(inner, 0.375, jnp.where(outer, 0.125, 0.0))


def build_tables(band, edge):
    k = lax.broadcasted_iota(jnp.int32, (256, 256), 0)
    n = lax.broadcasted_iota(jnp.int32, (256, 256), 1)
    own = tap_weight(k - (2 * n - 1))
    spill = jnp.logical_or(
        jnp.logical_and(n == 128, k == 255), jnp.logical_and(n == 255, k == 0)
    )
    table = jnp.where(n < 128, own, jnp.where(spill, 0.125, 0.0)).astype(BF16)
    band[0:256, :] = table
    band[256:512, :] = table
    k = lax.broadcasted_iota(jnp.int32, (128, 256), 0)
    n = lax.broadcasted_iota(jnp.int32, (128, 256), 1)
    right = jnp.where(k < 64, tap_weight(k - (2 * n - 1)), 0.0)
    left = jnp.where(k >= 64, tap_weight(k - (2 * n - 129)), 0.0)
    spill = jnp.logical_or(
        jnp.logical_and(n == 128, k == 127), jnp.logical_and(n == 255, k == 0)
    )
    table = jnp.where(
        n < 64, right, jnp.where(n < 128, left, jnp.where(spill, 0.125, 0.0))
    ).astype(BF16)
    edge[0:128, :] = table
    edge[128:256, :] = table


def pieces(x):
    high = x.astype(BF16)
    low = (x - high.astype(F32)).astype(BF16)
    return high, low


def land_of(words, tile):
    rows = words.shape[0]
    lane = lane_iota(rows)
    picked = jnp.take_along_axis(
        words, 4 * tile + lane // 32, axis=1, mode="promise_in_bounds"
    )
    return jnp.left_shift(picked, 31 - lane % 32) < 0


def wide(words):
    if words.shape[1] < LANES:
        words = jnp.concatenate([words] * (LANES // words.shape[1]), axis=1)
    return words


def dot(a, b):
    return jnp.dot(a, b, preferred_element_type=F32)


def first_across(field_tile, words, rows, s_num, s_den, r_num, r_den, band, tiles, store):
    words = wide(words)
    for tile in range(tiles):
        land = land_of(words, tile)
        masked = jnp.where(land, field_tile(tile), 0.0)
        high, low = pieces(masked)
        at = (tile // 2) * rows
        half = (tile % 2) * LANES
        s_num[at : at + rows, half : half + LANES] = high
        s_num[at : at + rows, 256 + half : 256 + half + LANES] = low
        s_den[at : at + rows, half : half + LANES] = jnp.where(land, 1.0, 0.0).astype(BF16)
    blocks = tiles // 2
    r_num[0 : blocks * rows, :] = dot(s_num[0 : blocks * rows, :], band[...])
    r_den[0 : blocks * rows, :] = dot(s_den[0 : blocks * rows, :], band[0:256, :])
    low_half = lane_iota(rows) < 64
    for which, ref in ((0, r_num), (1, r_den)):
        def spill(block):
            if block < 0 or block >= blocks:
                return jnp.zeros((rows, LANES), F32)
            return ref[block * rows : (block + 1) * rows, LANES : 2 * LANES]

        for block in range(blocks):
            own = ref[block * rows : (block + 1) * rows, 0:LANES]
            store(which, block, own + jnp.where(low_half, spill(block - 1), spill(block + 1)))
        store(which, blocks, jnp.where(low_half, spill(blocks - 1), spill(0)))


def kernel(
    field_hbm, words_hbm,
    v1, v2, v3, v4, stats,
    fld, wrd, fhal, whal, out_left, out_right, in_left, in_right, cornf, cornw,
    s_num, s_den, r_num, r_den, se_num, se_den, re_num, re_den,
    hn, hd, cosb, p1, d1, p2, d2, p3, d3,
    sx, sxe, rx, rxe, band, edge, msg_a, msg_b, slot_a, slot_b,
    load_sem, send_sem, recv_sem, a_send, a_recv, b_send, b_recv,
):
    n_rows, n_cols = lax.axis_size("rows"), lax.axis_size("cols")
    my_row, my_col = lax.axis_index("rows"), lax.axis_index("cols")
    rows, cols = fld.shape
    tiles = cols // LANES
    up, down = lax.rem(my_row + n_rows - 1, n_rows), lax.rem(my_row + 1, n_rows)
    left, right = lax.rem(my_col + n_cols - 1, n_cols), lax.rem(my_col + 1, n_cols)

    barrier = pltpu.get_barrier_semaphore()
    peers = [(my_row, lax.rem(my_col + s, n_cols)) for s in range(1, n_cols)]
    peers += [(lax.rem(my_row + s, n_rows), my_col) for s in range(1, n_rows)]
    peers += [(up, left), (up, right), (down, left), (down, right)]
    for peer in peers:
        pl.semaphore_signal(barrier, inc=1, device_id=peer, device_id_type=MESH)

    loads = []

    def load(src, dst):
        copy = pltpu.make_async_copy(src, dst, load_sem.at[len(loads)])
        copy.start()
        loads.append(copy)
        return copy

    load_words = load(words_hbm, wrd)
    load_strips = [
        load(field_hbm.at[:, 0:LANES], fld.at[:, 0:LANES]),
        load(field_hbm.at[:, cols - LANES : cols], fld.at[:, cols - LANES : cols]),
    ]
    chunks = rows // ROW_CHUNK
    order = [0, chunks - 1] + list(range(1, chunks - 1))
    load_chunk = {}
    for c in order:
        at = pl.ds(c * ROW_CHUNK, ROW_CHUNK)
        load_chunk[c] = load(
            field_hbm.at[at, LANES : cols - LANES], fld.at[at, LANES : cols - LANES]
        )

    build_tables(band, edge)
    for ref in (hn, hd, p1, d1, p2, d2, p3, d3):
        spare = PAD - HALO if ref.shape[1] == rows + 2 * PAD else HALO
        zeros = jnp.zeros((ref.shape[0], spare, LANES), F32)
        ref[:, 0:spare, :] = zeros
        ref[:, ref.shape[1] - spare :, :] = zeros

    sub = lax.broadcasted_iota(jnp.int32, (8, LANES), 0)
    global_row = my_row * rows - PAD + sub * LANES + lane_iota(8)
    latitude = ((global_row.astype(F32) + 0.5) / (rows * n_rows) - 0.5) * math.pi
    cosines = jnp.cos(latitude) * 0.125
    for q in range(cosb.shape[0] // LANES):
        row = jnp.broadcast_to(cosines[q : q + 1, :], (LANES, LANES))
        cosb[q * LANES : (q + 1) * LANES, :] = jnp.transpose(row)

    load_words.wait()
    for copy in load_strips:
        copy.wait()
    packed = rows // 8
    lane = lane_iota(packed)
    for out, tile, shift in ((out_left, 0, 0), (out_right, tiles - 1, HALO)):
        field_part = jnp.zeros((packed, LANES), F32)
        land_part = jnp.zeros((packed, LANES), F32)
        for g in range(8):
            at = slice(g * packed, (g + 1) * packed)
            values = fld[at, tile * LANES : (tile + 1) * LANES]
            land = jnp.where(land_of(wide(wrd[at, :]), tile), 1.0, 0.0)
            turn = (HALO * g + shift) % LANES
            if turn:
                values, land = pltpu.roll(values, turn, 1), pltpu.roll(land, turn, 1)
            here = lane // HALO == g
            field_part = jnp.where(here, values, field_part)
            land_part = jnp.where(here, land, land_part)
        out[0:packed, :] = field_part
        out[packed : 2 * packed, :] = land_part
    load_chunk[0].wait()
    if chunks > 1:
        load_chunk[chunks - 1].wait()

    pl.semaphore_wait(barrier, len(peers))

    sends = []

    def send(src, dst, row, col):
        i = len(sends)
        copy = pltpu.make_async_remote_copy(
            src_ref=src, dst_ref=dst, send_sem=send_sem.at[i], recv_sem=recv_sem.at[i],
            device_id=(row, col), device_id_type=MESH,
        )
        copy.start()
        sends.append(copy)

    top, bottom = slice(0, HALO), slice(rows - HALO, rows)
    last_tile = slice(cols - LANES, cols)
    send(out_left, in_right, my_row, left)
    send(out_right, in_left, my_row, right)
    send(fld.at[top, :], fhal.at[HALO : 2 * HALO, :], up, my_col)
    send(fld.at[bottom, :], fhal.at[0:HALO, :], down, my_col)
    send(wrd.at[top, :], whal.at[HALO : 2 * HALO, :], up, my_col)
    send(wrd.at[bottom, :], whal.at[0:HALO, :], down, my_col)
    send(fld.at[bottom, last_tile], cornf.at[0 * HALO : 1 * HALO, :], down, right)
    send(fld.at[bottom, 0:LANES], cornf.at[1 * HALO : 2 * HALO, :], down, left)
    send(fld.at[top, last_tile], cornf.at[2 * HALO : 3 * HALO, :], up, right)
    send(fld.at[top, 0:LANES], cornf.at[3 * HALO : 4 * HALO, :], up, left)
    send(wrd.at[bottom, :], cornw.at[0 * HALO : 1 * HALO, :], down, right)
    send(wrd.at[bottom, :], cornw.at[1 * HALO : 2 * HALO, :], down, left)
    send(wrd.at[top, :], cornw.at[2 * HALO : 3 * HALO, :], up, right)
    send(wrd.at[top, :], cornw.at[3 * HALO : 4 * HALO, :], up, left)

    for c in order[2:]:
        load_chunk[c].wait()

    def own_rows(c, carry):
        at = pl.multiple_of(c * ROW_CHUNK, ROW_CHUNK)

        def field_tile(tile):
            return fld[pl.ds(at, ROW_CHUNK), tile * LANES : (tile + 1) * LANES]

        def store(which, tile, value):
            ref = (hn, hd)[which]
            ref[tile, pl.ds(PAD + at, ROW_CHUNK), :] = value

        first_across(
            field_tile, wrd[pl.ds(at, ROW_CHUNK), :], ROW_CHUNK,
            s_num, s_den, r_num, r_den, band, tiles, store,
        )
        return carry

    lax.fori_loop(0, chunks, own_rows, 0)

    for copy in sends:
        copy.wait()

    def halo_store(which, tile, value):
        ref = (hn, hd)[which]
        ref[tile, PAD - HALO : PAD, :] = value[0:HALO, :]
        ref[tile, PAD + rows : PAD + rows + HALO, :] = value[HALO : 2 * HALO, :]

    first_across(
        lambda tile: fhal[:, tile * LANES : (tile + 1) * LANES], whal[...], 2 * HALO,
        s_num, s_den, r_num, r_den, band, tiles, halo_store,
    )

    def edge_store(at, count, field_value, land_value):
        high, low = pieces(field_value * land_value)
        se_num[at : at + count, 0:LANES] = high
        se_num[at : at + count, LANES : 2 * LANES] = low
        se_den[at : at + count, :] = land_value.astype(BF16)

    for g in range(8):
        parts = []
        for base in (0, packed):
            from_right = in_right[base : base + packed, :]
            from_left = in_left[base : base + packed, :]
            turn = (LANES - HALO * g) % LANES
            if turn:
                from_right = pltpu.roll(from_right, turn, 1)
            turn = (LANES - HALO - HALO * g) % LANES
            if turn:
                from_left = pltpu.roll(from_left, turn, 1)
            parts.append(
                jnp.where(
                    lane < HALO, from_right, jnp.where(lane >= LANES - HALO, from_left, 0.0)
                )
            )
        edge_store(g * packed, packed, parts[0], parts[1])
    lane16 = lane_iota(HALO)
    for side in range(2):
        l_at = slice(2 * side * HALO, (2 * side + 1) * HALO)
        r_at = slice((2 * side + 1) * HALO, (2 * side + 2) * HALO)
        is_right, is_left = lane16 < HALO, lane16 >= LANES - HALO
        value = jnp.where(is_right, cornf[r_at, :], jnp.where(is_left, cornf[l_at, :], 0.0))
        land_r = jnp.where(land_of(wide(cornw[r_at, :]), 0), 1.0, 0.0)
        land_l = jnp.where(land_of(wide(cornw[l_at, :]), tiles - 1), 1.0, 0.0)
        land = jnp.where(is_right, land_r, jnp.where(is_left, land_l, 0.0))
        edge_store(rows + side * HALO, HALO, value, land)
    re_num[...] = dot(se_num[...], edge[...])
    re_den[...] = dot(se_den[...], edge[0:128, :])
    out_tiles = tiles // 2

    def merge_edge(src, dst, count):
        low_half = lane_iota(count) < 64
        for result, ref in ((re_num, hn), (re_den, hd)):
            spill = result[pl.ds(src, count), LANES : 2 * LANES]
            here = pl.ds(dst, count)
            last = out_tiles - 1
            ref[0, here, :] = ref[0, here, :] + jnp.where(low_half, spill, 0.0)
            ref[last, here, :] = ref[last, here, :] + jnp.where(low_half, 0.0, spill)
            ref[out_tiles, here, :] = ref[out_tiles, here, :] + result[pl.ds(src, count), 0:LANES]

    def merge_own(c, carry):
        at = pl.multiple_of(c * ROW_CHUNK, ROW_CHUNK)
        merge_edge(at, PAD + at, ROW_CHUNK)
        return carry

    lax.fori_loop(0, chunks, merge_own, 0)
    merge_edge(rows, PAD - HALO, HALO)
    merge_edge(rows + HALO, PAD + rows, HALO)

    inside_top, inside_bottom = my_row > 0, my_row < n_rows - 1
    out_rows = rows // 2

    def finish(num, den):
        value = num / jnp.maximum(den, FLOOR)
        return value, den * value

    def level_one_rows(i0, tile, cosine):
        result = []
        for ref in (hn, hd):
            taps = [ref[tile, pl.ds(PAD + 2 * i0 - 1 + a, 8, stride=2), :] for a in range(4)]
            taps = [t * c for t, c in zip(taps, cosine)]
            result.append((taps[0] + taps[3]) + (taps[1] + taps[2]))
        return result

    def cosine_of(i0):
        taps = [cosb[pl.ds(PAD + 2 * i0 - 1 + a, 8, stride=2), :] for a in range(4)]
        return [taps[0], 3.0 * taps[1], 3.0 * taps[2], taps[3]]

    zero_sums = (
        jnp.zeros((8, LANES), F32), jnp.zeros((8, LANES), F32), jnp.full((8, LANES), -jnp.inf, F32)
    )

    def gather_sums(sums, value, product, cover):
        return (sums[0] + product, sums[1] + cover, jnp.maximum(sums[2], value))

    def level_one(c, sums):
        i0 = pl.multiple_of(c * 8, 8)
        cosine = cosine_of(i0)
        for tile in range(out_tiles + 1):
            at = slice(tile * LANES, (tile + 1) * LANES)
            num, den = level_one_rows(i0, tile, cosine)
            value, product = finish(num, den)
            p1[tile, pl.ds(PAD + i0, 8), :] = product
            d1[tile, pl.ds(PAD + i0, 8), :] = den
            if tile < out_tiles:
                v1[pl.ds(i0, 8), at] = value
                sums = gather_sums(sums, value, product, den)
        return sums

    all_sums = [lax.fori_loop(0, out_rows // 8, level_one, zero_sums)]
    for i0, keep in ((-8, inside_top), (out_rows, inside_bottom)):
        cosine = cosine_of(i0)
        for tile in range(out_tiles + 1):
            num, den = level_one_rows(i0, tile, cosine)
            value, product = finish(num, den)
            p1[tile, PAD + i0 : PAD + i0 + 8, :] = jnp.where(keep, product, 0.0)
            d1[tile, PAD + i0 : PAD + i0 + 8, :] = jnp.where(keep, den, 0.0)

    def next_level(pin, din, pout, dout, vout):
        out_rows, out_cols = vout.shape
        blocks = out_cols // LANES
        last_level = pout is None
        count = out_rows if last_level else out_rows + HALO

        def down_rows(ref, i0, size, tile):
            taps = [ref[tile, pl.ds(PAD + 2 * i0 - 1 + a, size, stride=2), :] for a in range(4)]
            return 0.125 * (taps[0] + taps[3]) + 0.375 * (taps[1] + taps[2])

        def put(which, tile, m0, value):
            high, low = pieces(value)
            if tile < 2 * blocks:
                base = (which * blocks + tile // 2) * count + m0
                half = (tile % 2) * LANES
                sx[pl.ds(base, 16), half : half + LANES] = high
                sx[pl.ds(base, 16), 256 + half : 256 + half + LANES] = low
            else:
                base = which * count + m0
                sxe[pl.ds(base, 16), 0:LANES] = high
                sxe[pl.ds(base, 16), LANES : 2 * LANES] = low

        def rows_step(c, carry):
            i0 = pl.multiple_of(c * 16, 16)
            for which, ref in ((0, pin), (1, din)):
                for tile in range(2 * blocks + 1):
                    value = jnp.concatenate(
                        [down_rows(ref, i0, 8, tile), down_rows(ref, i0 + 8, 8, tile)], axis=0
                    )
                    put(which, tile, i0, value)
            return carry

        lax.fori_loop(0, out_rows // 16, rows_step, 0)
        if not last_level:
            for which, ref in ((0, pin), (1, din)):
                for tile in range(2 * blocks + 1):
                    value = jnp.concatenate(
                        [down_rows(ref, -8, 8, tile), down_rows(ref, out_rows, 8, tile)], axis=0
                    )
                    put(which, tile, out_rows, value)
        total = 2 * blocks * count
        rx[0:total, :] = dot(sx[0:total, :], band[...])
        rxe[0 : 2 * count, :] = dot(sxe[0 : 2 * count, :], edge[...])
        low_half = lane_iota(8) < 64

        def across(m0, tile):
            result = []
            for which in range(2):
                def piece(block, half):
                    block = block % (blocks + 1)
                    at = slice(half * LANES, (half + 1) * LANES)
                    if block == blocks:
                        return rxe[pl.ds(which * count + m0, 8), at]
                    return rx[pl.ds((which * blocks + block) * count + m0, 8), at]

                result.append(
                    piece(tile, 0)
                    + jnp.where(low_half, piece(tile - 1, 1), piece(tile + 1, 1))
                )
            return result

        def finish_step(c, sums):
            i0 = pl.multiple_of(c * 8, 8)
            for tile in range(blocks + (0 if last_level else 1)):
                at = slice(tile * LANES, (tile + 1) * LANES)
                num, den = across(i0, tile)
                value, product = finish(num, den)
                if not last_level:
                    pout[tile, pl.ds(PAD + i0, 8), :] = product
                    dout[tile, pl.ds(PAD + i0, 8), :] = den
                if tile < blocks:
                    vout[pl.ds(i0, 8), at] = value
                    sums = gather_sums(sums, value, product, den)
            return sums

        sums = lax.fori_loop(0, out_rows // 8, finish_step, zero_sums)
        if not last_level:
            for m0, i0, keep in (
                (out_rows, -8, inside_top), (out_rows + 8, out_rows, inside_bottom)
            ):
                for tile in range(blocks + 1):
                    num, den = across(m0, tile)
                    value, product = finish(num, den)
                    pout[tile, PAD + i0 : PAD + i0 + 8, :] = jnp.where(keep, product, 0.0)
                    dout[tile, PAD + i0 : PAD + i0 + 8, :] = jnp.where(keep, den, 0.0)
        return sums

    all_sums.append(next_level(p1, d1, p2, d2, v2))
    all_sums.append(next_level(p2, d2, p3, d3, v3))
    all_sums.append(next_level(p3, d3, None, None, v4))

    lane = lane_iota(8)
    message = jnp.zeros((8, LANES), F32)

    def whole(x, op):
        return op(op(x, axis=0, keepdims=True), axis=1, keepdims=True)

    for level, sums in enumerate(all_sums):
        for place, (part, op) in enumerate(zip(sums, (jnp.sum, jnp.sum, jnp.max))):
            here = jnp.logical_and(sub == place, lane == level)
            message = jnp.where(here, whole(part, op), message)

    def exchange(message, buffer, slots, send_sems, recv_sems, index, count, device):
        buffer[...] = message
        slots[index] = message
        copies = []
        for s in range(1, count):
            peer = lax.rem(index + s, count)
            copy = pltpu.make_async_remote_copy(
                src_ref=buffer, dst_ref=slots.at[index],
                send_sem=send_sems.at[s], recv_sem=recv_sems.at[index],
                device_id=device(peer), device_id_type=MESH,
            )
            copy.start()
            copies.append(copy)
        for s in range(1, count):
            peer = lax.rem(index + s, count)
            pltpu.make_async_remote_copy(
                src_ref=buffer, dst_ref=slots.at[peer],
                send_sem=send_sems.at[s], recv_sem=recv_sems.at[peer],
                device_id=device(peer), device_id_type=MESH,
            ).wait_recv()
        added, largest = slots[0], slots[0]
        for i in range(1, count):
            added, largest = added + slots[i], jnp.maximum(largest, slots[i])
        for copy in copies:
            copy.wait_send()
        return jnp.where(sub == 2, largest, added)

    message = exchange(
        message, msg_a, slot_a, a_send, a_recv, my_col, n_cols, lambda peer: (my_row, peer)
    )
    message = exchange(
        message, msg_b, slot_b, b_send, b_recv, my_row, n_rows, lambda peer: (peer, my_col)
    )
    means = message[0:1, :] / (message[1:2, :] + EPS)
    stats[...] = jnp.where(sub == 0, means, jnp.where(sub == 1, message[2:3, :], 0.0))


def per_device(surface_field, land_words):
    rows, cols = surface_field.shape
    n_rows, n_cols = lax.axis_size("rows"), lax.axis_size("cols")
    words = land_words.shape[1]
    chunks = rows // ROW_CHUNK
    blocks = cols // 256
    packed = rows // 8

    def vmem(*shape, dtype=F32):
        return pltpu.VMEM(shape, dtype)

    level = [(rows >> l, cols >> l) for l in range(5)]
    scratch = [
        vmem(rows, cols), vmem(rows, words, dtype=jnp.int32),
        vmem(2 * HALO, cols), vmem(2 * HALO, words, dtype=jnp.int32),
        vmem(2 * packed, LANES), vmem(2 * packed, LANES),
        vmem(2 * packed, LANES), vmem(2 * packed, LANES),
        vmem(4 * HALO, LANES), vmem(4 * HALO, words, dtype=jnp.int32),
        vmem(blocks * ROW_CHUNK, 512, dtype=BF16), vmem(blocks * ROW_CHUNK, 256, dtype=BF16),
        vmem(blocks * ROW_CHUNK, 256), vmem(blocks * ROW_CHUNK, 256),
        vmem(rows + 2 * HALO, 256, dtype=BF16), vmem(rows + 2 * HALO, LANES, dtype=BF16),
        vmem(rows + 2 * HALO, 256), vmem(rows + 2 * HALO, 256),
        vmem(blocks + 1, rows + 2 * PAD, LANES), vmem(blocks + 1, rows + 2 * PAD, LANES),
        vmem(-(-(rows + 2 * PAD) // LANES) * LANES, LANES),
    ]
    for l in range(1, 4):
        scratch += [vmem(level[l][1] // LANES + 1, level[l][0] + 2 * PAD, LANES)] * 2
    count = level[2][0] + HALO
    inner_blocks = level[2][1] // LANES
    scratch += [
        vmem(2 * inner_blocks * count, 512, dtype=BF16), vmem(2 * count, 256, dtype=BF16),
        vmem(2 * inner_blocks * count, 256), vmem(2 * count, 256),
        vmem(512, 256, dtype=BF16), vmem(256, 256, dtype=BF16),
        vmem(8, LANES), vmem(8, LANES),
        vmem(n_cols, 8, LANES), vmem(n_rows, 8, LANES),
        pltpu.SemaphoreType.DMA((3 + chunks,)),
        pltpu.SemaphoreType.DMA((14,)), pltpu.SemaphoreType.DMA((14,)),
        pltpu.SemaphoreType.DMA((n_cols,)), pltpu.SemaphoreType.DMA((n_cols,)),
        pltpu.SemaphoreType.DMA((n_rows,)), pltpu.SemaphoreType.DMA((n_rows,)),
    ]
    out_shape = [jax.ShapeDtypeStruct(level[l], F32) for l in range(1, 5)]
    out_shape.append(jax.ShapeDtypeStruct((8, LANES), F32))
    v1, v2, v3, v4, stats = pl.pallas_call(
        kernel,
        out_shape=out_shape,
        in_specs=[pl.BlockSpec(memory_space=pl.ANY)] * 2,
        out_specs=[pl.BlockSpec(memory_space=pltpu.VMEM)] * 5,
        scratch_shapes=scratch,
        compiler_params=pltpu.CompilerParams(
            collective_id=0, has_side_effects=True, vmem_limit_bytes=48 * 1024 * 1024
        ),
    )(surface_field, land_words)
    return v1, v2, v3, v4, stats[0, :4], stats[1, :4]


def solution(mesh):
    spec = P("rows", "cols")
    return jax.shard_map(
        per_device, mesh=mesh, in_specs=(spec, spec),
        out_specs=(spec, spec, spec, spec, P(), P()), check_vma=False,
    )
```

profile of v0, /device:TPU:1, one launch (start us, length us, event | category | flops | bytes accessed | tf_op | source)
XLA Modules:
  0.0 37.2 jit_solution(5558045647673448238)
XLA Ops:
  0.6 1.0 %copy.8.words_hbm = s32[512,64]{1,0:T(8,128)S(1)} copy(s32[512,64]{0,1:T(8,128)} %param.3) | data formatting | bytes 262144 | tf_op args[1]
  1.7 0.0 copy-start
  1.7 2.2 %copy-done = f32[512,2048]{1,0:T(8,128)S(1)} copy-done((f32[512,2048]{1,0:T(8,128)S(1)}, f32[512,2048]{1,0:T(8,128)}, u32[]{:S(2)}) %copy-start) | copy-done | bytes 4194328
  3.9 29.9 %shard_map.73 = (f32[256,1024]{1,0:T(8,128)S(1)}, f32[128,512]{1,0:T(8,128)S(1)}, f32[64,256]{1,0:T(8,128)S(1)}, f32[32,128]{1,0:T(8,128)S(1)}, f32[8,128]{1,0:T(8,128)S(1)}) custom-call(f32[512,2048]{1,0:T(8,128)S(1)} %copy-done, s32[512,64]{1,0:T(8,128)S(1)} %copy.8.words_hbm), custom_call_target="tpu_custom_call" | custom-call | tf_op jit(solution)/shard_map/pallas_call | solution.py:541
  33.8 0.5 %slice_bitcast_fusion = (f32[4]{0:T(128)}, f32[4]{0:T(128)}) fusion(f32[8,128]{1,0:T(8,128)S(1)} %get-tuple-element.15), kind=kLoop, calls=%fused_computation | loop fusion | bytes 64 | tf_op jit(solution)/shard_map/squeeze | solution.py:551
  34.3 1.0 %copy.13 = f32[256,1024]{1,0:T(8,128)} copy(f32[256,1024]{1,0:T(8,128)S(1)} %get-tuple-element.24) | data formatting | bytes 2097152
  35.3 0.7 %copy.14 = f32[128,512]{1,0:T(8,128)} copy(f32[128,512]{1,0:T(8,128)S(1)} %get-tuple-element.25) | data formatting | bytes 524288
  36.0 0.6 %copy.15 = f32[64,256]{1,0:T(8,128)} copy(f32[64,256]{1,0:T(8,128)S(1)} %get-tuple-element.26) | data formatting | bytes 131072
  36.6 0.6 %copy.16 = f32[32,128]{1,0:T(8,128)} copy(f32[32,128]{1,0:T(8,128)S(1)} %get-tuple-element.27) | data formatting | bytes 32768
Async XLA Ops:
  1.7 2.2 %copy-start = (f32[512,2048]{1,0:T(8,128)S(1)}, f32[512,2048]{1,0:T(8,128)}, u32[]{:S(2)}) copy-start(f32[512,2048]{1,0:T(8,128)} %field_hbm.1) | copy-start | bytes 12582916
where the time goes:
time: 37.4 us; the launch traced here: 37.2 us
  Pallas kernels  29.9 us (80%)
  local copies, waits for them, and re-layouts  6.64 us (18%)
  between operations  0.66 us (2%)
    pallas_call x1, Pallas kernels, per_device(): pl.pallas_call(kernel, out_shape=out_shape, in_specs=[pl.BlockSpec(memory...  29.9 us
    unnamed x7, local copies, waits for them, and re-layouts  6.12 us

commit v1 on v0

--- a/solution.py
+++ b/solution.py
@@ -67,18 +67,11 @@
     return jnp.left_shift(picked, 31 - lane % 32) < 0
 
 
-def wide(words):
-    if words.shape[1] < LANES:
-        words = jnp.concatenate([words] * (LANES // words.shape[1]), axis=1)
-    return words
-
-
 def dot(a, b):
     return jnp.dot(a, b, preferred_element_type=F32)
 
 
 def first_across(field_tile, words, rows, s_num, s_den, r_num, r_den, band, tiles, store):
-    words = wide(words)
     for tile in range(tiles):
         land = land_of(words, tile)
         masked = jnp.where(land, field_tile(tile), 0.0)
@@ -107,7 +100,7 @@
 def kernel(
     field_hbm, words_hbm,
     v1, v2, v3, v4, stats,
-    fld, wrd, fhal, whal, out_left, out_right, in_left, in_right, cornf, cornw,
+    fld, wrd_cols, wrd, fhal, whal, out_left, out_right, in_left, in_right, cornf, cornw,
     s_num, s_den, r_num, r_den, se_num, se_den, re_num, re_den,
     hn, hd, cosb, p1, d1, p2, d2, p3, d3,
     sx, sxe, rx, rxe, band, edge, msg_a, msg_b, slot_a, slot_b,
@@ -135,7 +128,7 @@
         loads.append(copy)
         return copy
 
-    load_words = load(words_hbm, wrd)
+    load_words = load(words_hbm, wrd_cols)
     load_strips = [
         load(field_hbm.at[:, 0:LANES], fld.at[:, 0:LANES]),
         load(field_hbm.at[:, cols - LANES : cols], fld.at[:, cols - LANES : cols]),
@@ -159,12 +152,18 @@
     sub = lax.broadcasted_iota(jnp.int32, (8, LANES), 0)
     global_row = my_row * rows - PAD + sub * LANES + lane_iota(8)
     latitude = ((global_row.astype(F32) + 0.5) / (rows * n_rows) - 0.5) * math.pi
-    cosines = jnp.cos(latitude) * 0.125
+    on_globe = jnp.logical_and(global_row >= 0, global_row < rows * n_rows)
+    cosines = jnp.where(on_globe, jnp.cos(latitude) * 0.125, 0.0)
     for q in range(cosb.shape[0] // LANES):
         row = jnp.broadcast_to(cosines[q : q + 1, :], (LANES, LANES))
         cosb[q * LANES : (q + 1) * LANES, :] = jnp.transpose(row)
 
     load_words.wait()
+    copies_of = LANES // wrd_cols.shape[0]
+    for q in range(rows // LANES):
+        at = slice(q * LANES, (q + 1) * LANES)
+        wrd[at, :] = jnp.transpose(jnp.concatenate([wrd_cols[:, at]] * copies_of, axis=0))
+
     for copy in load_strips:
         copy.wait()
     packed = rows // 8
@@ -175,7 +174,7 @@
         for g in range(8):
             at = slice(g * packed, (g + 1) * packed)
             values = fld[at, tile * LANES : (tile + 1) * LANES]
-            land = jnp.where(land_of(wide(wrd[at, :]), tile), 1.0, 0.0)
+            land = jnp.where(land_of(wrd[at, :], tile), 1.0, 0.0)
             turn = (HALO * g + shift) % LANES
             if turn:
                 values, land = pltpu.roll(values, turn, 1), pltpu.roll(land, turn, 1)
@@ -281,8 +280,8 @@
         r_at = slice((2 * side + 1) * HALO, (2 * side + 2) * HALO)
         is_right, is_left = lane16 < HALO, lane16 >= LANES - HALO
         value = jnp.where(is_right, cornf[r_at, :], jnp.where(is_left, cornf[l_at, :], 0.0))
-        land_r = jnp.where(land_of(wide(cornw[r_at, :]), 0), 1.0, 0.0)
-        land_l = jnp.where(land_of(wide(cornw[l_at, :]), tiles - 1), 1.0, 0.0)
+        land_r = jnp.where(land_of(cornw[r_at, :], 0), 1.0, 0.0)
+        land_l = jnp.where(land_of(cornw[l_at, :], tiles - 1), 1.0, 0.0)
         land = jnp.where(is_right, land_r, jnp.where(is_left, land_l, 0.0))
         edge_store(rows + side * HALO, HALO, value, land)
     re_num[...] = dot(se_num[...], edge[...])
@@ -448,16 +447,15 @@
     all_sums.append(next_level(p2, d2, p3, d3, v3))
     all_sums.append(next_level(p3, d3, None, None, v4))
 
-    lane = lane_iota(8)
-    message = jnp.zeros((8, LANES), F32)
+    lane = lane_iota(1)
+    message = jnp.zeros((1, LANES), F32)
 
     def whole(x, op):
         return op(op(x, axis=0, keepdims=True), axis=1, keepdims=True)
 
     for level, sums in enumerate(all_sums):
         for place, (part, op) in enumerate(zip(sums, (jnp.sum, jnp.sum, jnp.max))):
-            here = jnp.logical_and(sub == place, lane == level)
-            message = jnp.where(here, whole(part, op), message)
+            message = jnp.where(lane == 4 * place + level, whole(part, op), message)
 
     def exchange(message, buffer, slots, send_sems, recv_sems, index, count, device):
         buffer[...] = message
@@ -484,16 +482,44 @@
             added, largest = added + slots[i], jnp.maximum(largest, slots[i])
         for copy in copies:
             copy.wait_send()
-        return jnp.where(sub == 2, largest, added)
-
+        return jnp.where(lane < 8, added, largest)
+
+    message = exchange(
+        message, msg_b, slot_b, b_send, b_recv, my_row, n_rows, lambda peer: (peer, my_col)
+    )
     message = exchange(
         message, msg_a, slot_a, a_send, a_recv, my_col, n_cols, lambda peer: (my_row, peer)
     )
-    message = exchange(
-        message, msg_b, slot_b, b_send, b_recv, my_row, n_rows, lambda peer: (peer, my_col)
-    )
-    means = message[0:1, :] / (message[1:2, :] + EPS)
-    stats[...] = jnp.where(sub == 0, means, jnp.where(sub == 1, message[2:3, :], 0.0))
+    wide = jnp.broadcast_to(message, (8, LANES))
+    covers = pltpu.roll(wide, LANES - 4, 1)
+    maxima = pltpu.roll(wide, LANES - 8, 1)
+    stats[...] = jnp.where(sub == 0, wide / (covers + EPS), maxima)
+
+
+def copy_out(v1, v2, v3, v4, stats):
+    def body(*refs):
+        ins, outs, means, maxima, sem = refs[:5], refs[5:9], refs[9], refs[10], refs[11]
+        copies = []
+        for i in range(4):
+            copy = pltpu.make_async_copy(ins[i], outs[i], sem.at[i])
+            copy.start()
+            copies.append(copy)
+        for i in range(4):
+            means[i] = ins[4][0, i]
+            maxima[i] = ins[4][1, i]
+        for copy in copies:
+            copy.wait()
+
+    shapes = [jax.ShapeDtypeStruct(v.shape, F32) for v in (v1, v2, v3, v4)]
+    shapes += [jax.ShapeDtypeStruct((4,), F32)] * 2
+    return pl.pallas_call(
+        body,
+        out_shape=shapes,
+        in_specs=[pl.BlockSpec(memory_space=pltpu.VMEM)] * 5,
+        out_specs=[pl.BlockSpec(memory_space=pl.ANY)] * 4
+        + [pl.BlockSpec(memory_space=pltpu.SMEM)] * 2,
+        scratch_shapes=[pltpu.SemaphoreType.DMA((4,))],
+    )(*[pltpu.with_memory_space_constraint(x, pltpu.VMEM) for x in (v1, v2, v3, v4, stats)])
 
 
 def per_device(surface_field, land_words):
@@ -509,11 +535,11 @@
 
     level = [(rows >> l, cols >> l) for l in range(5)]
     scratch = [
-        vmem(rows, cols), vmem(rows, words, dtype=jnp.int32),
-        vmem(2 * HALO, cols), vmem(2 * HALO, words, dtype=jnp.int32),
+        vmem(rows, cols), vmem(words, rows, dtype=jnp.int32), vmem(rows, LANES, dtype=jnp.int32),
+        vmem(2 * HALO, cols), vmem(2 * HALO, LANES, dtype=jnp.int32),
         vmem(2 * packed, LANES), vmem(2 * packed, LANES),
         vmem(2 * packed, LANES), vmem(2 * packed, LANES),
-        vmem(4 * HALO, LANES), vmem(4 * HALO, words, dtype=jnp.int32),
+        vmem(4 * HALO, LANES), vmem(4 * HALO, LANES, dtype=jnp.int32),
         vmem(blocks * ROW_CHUNK, 512, dtype=BF16), vmem(blocks * ROW_CHUNK, 256, dtype=BF16),
         vmem(blocks * ROW_CHUNK, 256), vmem(blocks * ROW_CHUNK, 256),
         vmem(rows + 2 * HALO, 256, dtype=BF16), vmem(rows + 2 * HALO, LANES, dtype=BF16),
@@ -529,15 +555,15 @@
         vmem(2 * inner_blocks * count, 512, dtype=BF16), vmem(2 * count, 256, dtype=BF16),
         vmem(2 * inner_blocks * count, 256), vmem(2 * count, 256),
         vmem(512, 256, dtype=BF16), vmem(256, 256, dtype=BF16),
-        vmem(8, LANES), vmem(8, LANES),
-        vmem(n_cols, 8, LANES), vmem(n_rows, 8, LANES),
+        vmem(1, LANES), vmem(1, LANES),
+        vmem(n_cols, 1, LANES), vmem(n_rows, 1, LANES),
         pltpu.SemaphoreType.DMA((3 + chunks,)),
         pltpu.SemaphoreType.DMA((14,)), pltpu.SemaphoreType.DMA((14,)),
         pltpu.SemaphoreType.DMA((n_cols,)), pltpu.SemaphoreType.DMA((n_cols,)),
         pltpu.SemaphoreType.DMA((n_rows,)), pltpu.SemaphoreType.DMA((n_rows,)),
     ]
-    out_shape = [jax.ShapeDtypeStruct(level[l], F32) for l in range(1, 5)]
-    out_shape.append(jax.ShapeDtypeStruct((8, LANES), F32))
+    out_shape = [pltpu.VMEM(level[l], F32) for l in range(1, 5)]
+    out_shape.append(pltpu.VMEM((8, LANES), F32))
     v1, v2, v3, v4, stats = pl.pallas_call(
         kernel,
         out_shape=out_shape,
@@ -547,8 +573,11 @@
         compiler_params=pltpu.CompilerParams(
             collective_id=0, has_side_effects=True, vmem_limit_bytes=48 * 1024 * 1024
         ),
-    )(surface_field, land_words)
-    return v1, v2, v3, v4, stats[0, :4], stats[1, :4]
+    )(
+        pltpu.with_memory_space_constraint(surface_field, pltpu.HBM),
+        pltpu.with_memory_space_constraint(land_words.T, pltpu.HBM),
+    )
+    return copy_out(v1, v2, v3, v4, stats)
 
 
 def solution(mesh):

time: 37.4 us -> 30.6 us (0.82)
  local copies, waits for them, and re-layouts: 6.64 us -> 0 us
    unnamed x7 -> x0, local copies, waits for them, and re-layouts: 6.12 us -> none
    pallas_call x1, Pallas kernels: 29.9 us -> 28.1 us  [per_device(): pl.pallas_call(kernel, out_shape=out_shape, in_specs=[pl.BlockSpec(memory...]
    pallas_call x0 -> x1, Pallas kernels: none -> 1.63 us  [copy_out(): pl.pallas_call(body, out_shape=shapes, in_specs=[pl.BlockSpec(memory_spac...]
    squeeze x1 -> x0, local copies, waits for them, and re-layouts: 0.52 us -> none  [per_device(): return (v1, v2, v3, v4, stats[0, :4], stats[1, :4])]
where the time goes in v1:
time: 30.6 us; the launch traced here: 30.3 us
  Pallas kernels  29.7 us (97%)
  between operations  0.64 us (2%)
    pallas_call x1, Pallas kernels, per_device(): pl.pallas_call(kernel, out_shape=out_shape, in_specs=[pl.BlockSpec(memory...  28.1 us
    pallas_call x1, Pallas kernels, copy_out(): pl.pallas_call(body, out_shape=shapes, in_specs=[pl.BlockSpec(memory_spac...  1.63 us

profile of v1, /device:TPU:1, one launch (start us, length us, event | category | flops | bytes accessed | tf_op | source)
XLA Modules:
  0.0 30.3 jit_solution(2209750890474313095)
XLA Ops:
  0.6 28.1 %shard_map.73 = (f32[256,1024]{1,0:T(8,128)S(1)}, f32[128,512]{1,0:T(8,128)S(1)}, f32[64,256]{1,0:T(8,128)S(1)}, f32[32,128]{1,0:T(8,128)S(1)}, f32[8,128]{1,0:T(8,128)S(1)}) custom-call(f32[512,2048]{1,0:T(8,128)} %field_hbm.1, s32[64,512]{1,0:T(8,128)} %bitcast.1), custom_call_target="tpu_custom_call" | custom-call | tf_op jit(solution)/shard_map/pallas_call | solution.py:567
  28.7 1.6 %shard_map.74 = (f32[256,1024]{1,0:T(8,128)}, f32[128,512]{1,0:T(8,128)}, f32[64,256]{1,0:T(8,128)}, f32[32,128]{1,0:T(8,128)}, f32[4]{0:T(128)}, /*index=5*/f32[4]{0:T(128)}) custom-call(f32[256,1024]{1,0:T(8,128)S(1)} %get-tuple-element.11.refs_0_, f32[128,512]{1,0:T(8,128)S(1)} %get-tuple-element.12.refs_1_, f32[64,256]{1,0:T(8,128)S(1)} %get-tuple-element.13.refs_2_, ...), custom_call_target="tpu_custom_call" | custom-call | tf_op jit(solution)/shard_map/pallas_call | solution.py:515

commit v2 on v1

--- a/solution.py
+++ b/solution.py
@@ -35,9 +35,9 @@
     spill = jnp.logical_or(
         jnp.logical_and(n == 128, k == 255), jnp.logical_and(n == 255, k == 0)
     )
-    table = jnp.where(n < 128, own, jnp.where(spill, 0.125, 0.0)).astype(BF16)
-    band[0:256, :] = table
-    band[256:512, :] = table
+    table = jnp.where(n < 128, own, jnp.where(spill, 0.125, 0.0))
+    band[0:256, :] = table.astype(BF16)
+    band[256:512, :] = table.astype(BF16)
     k = lax.broadcasted_iota(jnp.int32, (128, 256), 0)
     n = lax.broadcasted_iota(jnp.int32, (128, 256), 1)
     right = jnp.where(k < 64, tap_weight(k - (2 * n - 1)), 0.0)
@@ -71,16 +71,19 @@
     return jnp.dot(a, b, preferred_element_type=F32)
 
 
-def first_across(field_tile, words, rows, s_num, s_den, r_num, r_den, band, tiles, store):
+def mask_step(field_tile, words, rows, s_num, s_den, tiles):
     for tile in range(tiles):
         land = land_of(words, tile)
         masked = jnp.where(land, field_tile(tile), 0.0)
-        high, low = pieces(masked)
         at = (tile // 2) * rows
         half = (tile % 2) * LANES
+        high, low = pieces(masked)
         s_num[at : at + rows, half : half + LANES] = high
         s_num[at : at + rows, 256 + half : 256 + half + LANES] = low
         s_den[at : at + rows, half : half + LANES] = jnp.where(land, 1.0, 0.0).astype(BF16)
+
+
+def across_step(rows, s_num, s_den, r_num, r_den, band, tiles, store):
     blocks = tiles // 2
     r_num[0 : blocks * rows, :] = dot(s_num[0 : blocks * rows, :], band[...])
     r_den[0 : blocks * rows, :] = dot(s_den[0 : blocks * rows, :], band[0:256, :])
@@ -97,11 +100,16 @@
         store(which, blocks, jnp.where(low_half, spill(blocks - 1), spill(0)))
 
 
+def first_across(field_tile, words, rows, s_num, s_den, r_num, r_den, band, tiles, store):
+    mask_step(field_tile, words, rows, s_num, s_den, tiles)
+    across_step(rows, s_num, s_den, r_num, r_den, band, tiles, store)
+
+
 def kernel(
     field_hbm, words_hbm,
     v1, v2, v3, v4, stats,
     fld, wrd_cols, wrd, fhal, whal, out_left, out_right, in_left, in_right, cornf, cornw,
-    s_num, s_den, r_num, r_den, se_num, se_den, re_num, re_den,
+    s_num, s_den, r_num, r_den, s_num2, s_den2, r_num2, r_den2, se_num, se_den, re_num, re_den,
     hn, hd, cosb, p1, d1, p2, d2, p3, d3,
     sx, sxe, rx, rxe, band, edge, msg_a, msg_b, slot_a, slot_b,
     load_sem, send_sem, recv_sem, a_send, a_recv, b_send, b_recv,
@@ -220,42 +228,110 @@
     for c in order[2:]:
         load_chunk[c].wait()
 
-    def own_rows(c, carry):
-        at = pl.multiple_of(c * ROW_CHUNK, ROW_CHUNK)
-
+    sets = ((s_num, s_den, r_num, r_den), (s_num2, s_den2, r_num2, r_den2))
+
+    def own_mask(at, which):
         def field_tile(tile):
             return fld[pl.ds(at, ROW_CHUNK), tile * LANES : (tile + 1) * LANES]
 
+        mask_step(
+            field_tile, wrd[pl.ds(at, ROW_CHUNK), :], ROW_CHUNK, *sets[which][0:2], tiles
+        )
+
+    def own_across(at, which):
         def store(which, tile, value):
             ref = (hn, hd)[which]
             ref[tile, pl.ds(PAD + at, ROW_CHUNK), :] = value
 
-        first_across(
-            field_tile, wrd[pl.ds(at, ROW_CHUNK), :], ROW_CHUNK,
-            s_num, s_den, r_num, r_den, band, tiles, store,
-        )
-        return carry
-
-    lax.fori_loop(0, chunks, own_rows, 0)
-
-    for copy in sends:
+        across_step(ROW_CHUNK, *sets[which], band, tiles, store)
+
+    own_mask(0, 0)
+    for c in range(chunks):
+        if c + 1 < chunks:
+            own_mask((c + 1) * ROW_CHUNK, (c + 1) % 2)
+        own_across(c * ROW_CHUNK, c % 2)
+
+    inside_top, inside_bottom = my_row > 0, my_row < n_rows - 1
+    out_rows, out_tiles = rows // 2, tiles // 2
+
+    def finish(num, den):
+        value = num / jnp.maximum(den, FLOOR)
+        return value, den * value
+
+    zero_sums = (
+        jnp.zeros((8, LANES), F32), jnp.zeros((8, LANES), F32), jnp.full((8, LANES), -jnp.inf, F32)
+    )
+
+    def gather_sums(sums, value, product, cover):
+        return (sums[0] + product, sums[1] + cover, jnp.maximum(sums[2], value))
+
+    def level_one_rows(i0, tile, cosine):
+        result = []
+        for ref in (hn, hd):
+            taps = [ref[tile, pl.ds(PAD + 2 * i0 - 1 + a, 8, stride=2), :] for a in range(4)]
+            taps = [t * c for t, c in zip(taps, cosine)]
+            result.append((taps[0] + taps[3]) + (taps[1] + taps[2]))
+        return result
+
+    def cosine_of(i0):
+        taps = [cosb[pl.ds(PAD + 2 * i0 - 1 + a, 8, stride=2), :] for a in range(4)]
+        return [taps[0], 3.0 * taps[1], 3.0 * taps[2], taps[3]]
+
+    def level_one_own(i0, which_tiles, sums):
+        cosine = cosine_of(i0)
+        for tile in which_tiles:
+            num, den = level_one_rows(i0, tile, cosine)
+            value, product = finish(num, den)
+            p1[tile, pl.ds(PAD + i0, 8), :] = product
+            d1[tile, pl.ds(PAD + i0, 8), :] = den
+            if tile < out_tiles:
+                v1[pl.ds(i0, 8), tile * LANES : (tile + 1) * LANES] = value
+                sums = gather_sums(sums, value, product, den)
+        return sums
+
+    def level_one_inner(which_tiles, sums):
+        def pair(c, sums):
+            i0 = pl.multiple_of(8 + c * 16, 8)
+            sums = level_one_own(i0, which_tiles, sums)
+            return level_one_own(i0 + 8, which_tiles, sums)
+
+        return lax.fori_loop(0, out_rows // 16 - 1, pair, sums)
+
+    def level_one_beyond(i0, keep):
+        cosine = cosine_of(i0)
+        for tile in range(out_tiles + 1):
+            num, den = level_one_rows(i0, tile, cosine)
+            value, product = finish(num, den)
+            p1[tile, PAD + i0 : PAD + i0 + 8, :] = jnp.where(keep, product, 0.0)
+            d1[tile, PAD + i0 : PAD + i0 + 8, :] = jnp.where(keep, den, 0.0)
+
+    sums_one = level_one_inner(range(1, out_tiles - 1), zero_sums)
+
+    for copy in sends[0:2]:
         copy.wait()
-
-    def halo_store(which, tile, value):
-        ref = (hn, hd)[which]
-        ref[tile, PAD - HALO : PAD, :] = value[0:HALO, :]
-        ref[tile, PAD + rows : PAD + rows + HALO, :] = value[HALO : 2 * HALO, :]
-
-    first_across(
-        lambda tile: fhal[:, tile * LANES : (tile + 1) * LANES], whal[...], 2 * HALO,
-        s_num, s_den, r_num, r_den, band, tiles, halo_store,
-    )
 
     def edge_store(at, count, field_value, land_value):
         high, low = pieces(field_value * land_value)
         se_num[at : at + count, 0:LANES] = high
         se_num[at : at + count, LANES : 2 * LANES] = low
         se_den[at : at + count, :] = land_value.astype(BF16)
+
+    def edge_dot(at, count):
+        here = slice(at, at + count)
+        re_num[here, :] = dot(se_num[here, :], edge[...])
+        re_den[here, :] = dot(se_den[here, :], edge[0:128, :])
+
+    def merge_edge(src, dst, count):
+        low_half = lane_iota(count) < 64
+        for result, ref in ((re_num, hn), (re_den, hd)):
+            spill = result[src : src + count, LANES : 2 * LANES]
+            here = slice(dst, dst + count)
+            last = out_tiles - 1
+            ref[0, here, :] = ref[0, here, :] + jnp.where(low_half, spill, 0.0)
+            ref[last, here, :] = ref[last, here, :] + jnp.where(low_half, 0.0, spill)
+            ref[out_tiles, here, :] = (
+                ref[out_tiles, here, :] + result[src : src + count, 0:LANES]
+            )
 
     for g in range(8):
         parts = []
@@ -274,6 +350,22 @@
                 )
             )
         edge_store(g * packed, packed, parts[0], parts[1])
+    edge_dot(0, rows)
+    merge_edge(0, PAD, rows)
+    sums_one = level_one_inner((0, out_tiles - 1, out_tiles), sums_one)
+
+    for copy in sends[2:]:
+        copy.wait()
+
+    def halo_store(which, tile, value):
+        ref = (hn, hd)[which]
+        ref[tile, PAD - HALO : PAD, :] = value[0:HALO, :]
+        ref[tile, PAD + rows : PAD + rows + HALO, :] = value[HALO : 2 * HALO, :]
+
+    first_across(
+        lambda tile: fhal[:, tile * LANES : (tile + 1) * LANES], whal[...], 2 * HALO,
+        s_num, s_den, r_num, r_den, band, tiles, halo_store,
+    )
     lane16 = lane_iota(HALO)
     for side in range(2):
         l_at = slice(2 * side * HALO, (2 * side + 1) * HALO)
@@ -284,163 +376,86 @@
         land_l = jnp.where(land_of(cornw[l_at, :], tiles - 1), 1.0, 0.0)
         land = jnp.where(is_right, land_r, jnp.where(is_left, land_l, 0.0))
         edge_store(rows + side * HALO, HALO, value, land)
-    re_num[...] = dot(se_num[...], edge[...])
-    re_den[...] = dot(se_den[...], edge[0:128, :])
-    out_tiles = tiles // 2
-
-    def merge_edge(src, dst, count):
-        low_half = lane_iota(count) < 64
-        for result, ref in ((re_num, hn), (re_den, hd)):
-            spill = result[pl.ds(src, count), LANES : 2 * LANES]
-            here = pl.ds(dst, count)
-            last = out_tiles - 1
-            ref[0, here, :] = ref[0, here, :] + jnp.where(low_half, spill, 0.0)
-            ref[last, here, :] = ref[last, here, :] + jnp.where(low_half, 0.0, spill)
-            ref[out_tiles, here, :] = ref[out_tiles, here, :] + result[pl.ds(src, count), 0:LANES]
-
-    def merge_own(c, carry):
-        at = pl.multiple_of(c * ROW_CHUNK, ROW_CHUNK)
-        merge_edge(at, PAD + at, ROW_CHUNK)
-        return carry
-
-    lax.fori_loop(0, chunks, merge_own, 0)
+    edge_dot(rows, 2 * HALO)
     merge_edge(rows, PAD - HALO, HALO)
     merge_edge(rows + HALO, PAD + rows, HALO)
-
-    inside_top, inside_bottom = my_row > 0, my_row < n_rows - 1
-    out_rows = rows // 2
-
-    def finish(num, den):
-        value = num / jnp.maximum(den, FLOOR)
-        return value, den * value
-
-    def level_one_rows(i0, tile, cosine):
-        result = []
-        for ref in (hn, hd):
-            taps = [ref[tile, pl.ds(PAD + 2 * i0 - 1 + a, 8, stride=2), :] for a in range(4)]
-            taps = [t * c for t, c in zip(taps, cosine)]
-            result.append((taps[0] + taps[3]) + (taps[1] + taps[2]))
-        return result
-
-    def cosine_of(i0):
-        taps = [cosb[pl.ds(PAD + 2 * i0 - 1 + a, 8, stride=2), :] for a in range(4)]
-        return [taps[0], 3.0 * taps[1], 3.0 * taps[2], taps[3]]
-
-    zero_sums = (
-        jnp.zeros((8, LANES), F32), jnp.zeros((8, LANES), F32), jnp.full((8, LANES), -jnp.inf, F32)
-    )
-
-    def gather_sums(sums, value, product, cover):
-        return (sums[0] + product, sums[1] + cover, jnp.maximum(sums[2], value))
-
-    def level_one(c, sums):
-        i0 = pl.multiple_of(c * 8, 8)
-        cosine = cosine_of(i0)
-        for tile in range(out_tiles + 1):
-            at = slice(tile * LANES, (tile + 1) * LANES)
-            num, den = level_one_rows(i0, tile, cosine)
-            value, product = finish(num, den)
-            p1[tile, pl.ds(PAD + i0, 8), :] = product
-            d1[tile, pl.ds(PAD + i0, 8), :] = den
-            if tile < out_tiles:
-                v1[pl.ds(i0, 8), at] = value
-                sums = gather_sums(sums, value, product, den)
-        return sums
-
-    all_sums = [lax.fori_loop(0, out_rows // 8, level_one, zero_sums)]
-    for i0, keep in ((-8, inside_top), (out_rows, inside_bottom)):
-        cosine = cosine_of(i0)
-        for tile in range(out_tiles + 1):
-            num, den = level_one_rows(i0, tile, cosine)
-            value, product = finish(num, den)
-            p1[tile, PAD + i0 : PAD + i0 + 8, :] = jnp.where(keep, product, 0.0)
-            d1[tile, PAD + i0 : PAD + i0 + 8, :] = jnp.where(keep, den, 0.0)
+    for i0 in (0, out_rows - 8):
+        sums_one = level_one_own(i0, range(out_tiles + 1), sums_one)
+    level_one_beyond(-8, inside_top)
+    level_one_beyond(out_rows, inside_bottom)
+    all_sums = [sums_one]
 
     def next_level(pin, din, pout, dout, vout):
         out_rows, out_cols = vout.shape
         blocks = out_cols // LANES
         last_level = pout is None
-        count = out_rows if last_level else out_rows + HALO
-
-        def down_rows(ref, i0, size, tile):
-            taps = [ref[tile, pl.ds(PAD + 2 * i0 - 1 + a, size, stride=2), :] for a in range(4)]
+        groups = [(i0, i0 + 8) for i0 in range(0, out_rows, 16)]
+        parts = [groups[i : i + 4] for i in range(0, len(groups), 4)]
+        if not last_level:
+            parts.append([(-8, out_rows)])
+        low_half = lane_iota(8) < 64
+
+        def down_rows(ref, i0, tile):
+            taps = [ref[tile, pl.ds(PAD + 2 * i0 - 1 + a, 8, stride=2), :] for a in range(4)]
             return 0.125 * (taps[0] + taps[3]) + 0.375 * (taps[1] + taps[2])
 
-        def put(which, tile, m0, value):
-            high, low = pieces(value)
-            if tile < 2 * blocks:
-                base = (which * blocks + tile // 2) * count + m0
-                half = (tile % 2) * LANES
-                sx[pl.ds(base, 16), half : half + LANES] = high
-                sx[pl.ds(base, 16), 256 + half : 256 + half + LANES] = low
-            else:
-                base = which * count + m0
-                sxe[pl.ds(base, 16), 0:LANES] = high
-                sxe[pl.ds(base, 16), LANES : 2 * LANES] = low
-
-        def rows_step(c, carry):
-            i0 = pl.multiple_of(c * 16, 16)
-            for which, ref in ((0, pin), (1, din)):
-                for tile in range(2 * blocks + 1):
-                    value = jnp.concatenate(
-                        [down_rows(ref, i0, 8, tile), down_rows(ref, i0 + 8, 8, tile)], axis=0
-                    )
-                    put(which, tile, i0, value)
-            return carry
-
-        lax.fori_loop(0, out_rows // 16, rows_step, 0)
-        if not last_level:
-            for which, ref in ((0, pin), (1, din)):
-                for tile in range(2 * blocks + 1):
-                    value = jnp.concatenate(
-                        [down_rows(ref, -8, 8, tile), down_rows(ref, out_rows, 8, tile)], axis=0
-                    )
-                    put(which, tile, out_rows, value)
-        total = 2 * blocks * count
-        rx[0:total, :] = dot(sx[0:total, :], band[...])
-        rxe[0 : 2 * count, :] = dot(sxe[0 : 2 * count, :], edge[...])
-        low_half = lane_iota(8) < 64
-
-        def across(m0, tile):
-            result = []
-            for which in range(2):
-                def piece(block, half):
-                    block = block % (blocks + 1)
-                    at = slice(half * LANES, (half + 1) * LANES)
-                    if block == blocks:
-                        return rxe[pl.ds(which * count + m0, 8), at]
-                    return rx[pl.ds((which * blocks + block) * count + m0, 8), at]
-
-                result.append(
-                    piece(tile, 0)
-                    + jnp.where(low_half, piece(tile - 1, 1), piece(tile + 1, 1))
-                )
-            return result
-
-        def finish_step(c, sums):
-            i0 = pl.multiple_of(c * 8, 8)
-            for tile in range(blocks + (0 if last_level else 1)):
-                at = slice(tile * LANES, (tile + 1) * LANES)
-                num, den = across(i0, tile)
-                value, product = finish(num, den)
-                if not last_level:
-                    pout[tile, pl.ds(PAD + i0, 8), :] = product
-                    dout[tile, pl.ds(PAD + i0, 8), :] = den
-                if tile < blocks:
-                    vout[pl.ds(i0, 8), at] = value
-                    sums = gather_sums(sums, value, product, den)
-            return sums
-
-        sums = lax.fori_loop(0, out_rows // 8, finish_step, zero_sums)
-        if not last_level:
-            for m0, i0, keep in (
-                (out_rows, -8, inside_top), (out_rows + 8, out_rows, inside_bottom)
-            ):
-                for tile in range(blocks + 1):
-                    num, den = across(m0, tile)
-                    value, product = finish(num, den)
-                    pout[tile, PAD + i0 : PAD + i0 + 8, :] = jnp.where(keep, product, 0.0)
-                    dout[tile, PAD + i0 : PAD + i0 + 8, :] = jnp.where(keep, den, 0.0)
+        sums, base, base_e = zero_sums, 0, 0
+        for part in parts:
+            count = 16 * len(part)
+            for g, pair in enumerate(part):
+                for which, ref in ((0, pin), (1, din)):
+                    for tile in range(2 * blocks + 1):
+                        value = jnp.concatenate(
+                            [down_rows(ref, i0, tile) for i0 in pair], axis=0
+                        )
+                        high, low = pieces(value)
+                        if tile < 2 * blocks:
+                            at = base + (which * blocks + tile // 2) * count + 16 * g
+                            half = (tile % 2) * LANES
+                            sx[at : at + 16, half : half + LANES] = high
+                            sx[at : at + 16, 256 + half : 256 + half + LANES] = low
+                        else:
+                            at = base_e + which * count + 16 * g
+                            sxe[at : at + 16, 0:LANES] = high
+                            sxe[at : at + 16, LANES : 2 * LANES] = low
+            total = 2 * blocks * count
+            rx[base : base + total, :] = dot(sx[base : base + total, :], band[...])
+            rxe[base_e : base_e + 2 * count, :] = dot(
+                sxe[base_e : base_e + 2 * count, :], edge[...]
+            )
+            starts = [i0 for pair in part for i0 in pair]
+            for m, i0 in enumerate(starts):
+                beyond = i0 < 0 or i0 >= out_rows
+                keep = inside_top if i0 < 0 else inside_bottom
+                for tile in range(blocks + (0 if last_level else 1)):
+                    both = []
+                    for which in range(2):
+                        def piece(block, half, which=which):
+                            block = block % (blocks + 1)
+                            lanes = slice(half * LANES, (half + 1) * LANES)
+                            if block == blocks:
+                                at = base_e + which * count + 8 * m
+                                return rxe[at : at + 8, lanes]
+                            at = base + (which * blocks + block) * count + 8 * m
+                            return rx[at : at + 8, lanes]
+
+                        both.append(
+                            piece(tile, 0)
+                            + jnp.where(low_half, piece(tile - 1, 1), piece(tile + 1, 1))
+                        )
+                    value, product = finish(*both)
+                    if beyond:
+                        pout[tile, PAD + i0 : PAD + i0 + 8, :] = jnp.where(keep, product, 0.0)
+                        dout[tile, PAD + i0 : PAD + i0 + 8, :] = jnp.where(keep, both[1], 0.0)
+                        continue
+                    if not last_level:
+                        pout[tile, PAD + i0 : PAD + i0 + 8, :] = product
+                        dout[tile, PAD + i0 : PAD + i0 + 8, :] = both[1]
+                    if tile < blocks:
+                        vout[i0 : i0 + 8, tile * LANES : (tile + 1) * LANES] = value
+                        sums = gather_sums(sums, value, product, both[1])
+            base += total
+            base_e += 2 * count
         return sums
 
     all_sums.append(next_level(p1, d1, p2, d2, v2))
@@ -500,8 +515,11 @@
     def body(*refs):
         ins, outs, means, maxima, sem = refs[:5], refs[5:9], refs[9], refs[10], refs[11]
         copies = []
-        for i in range(4):
-            copy = pltpu.make_async_copy(ins[i], outs[i], sem.at[i])
+        steps = ins[0].shape[0] // 8
+        parts = [(0, pl.ds(k * steps, steps)) for k in range(8)]
+        parts += [(i, pl.ds(0, ins[i].shape[0])) for i in range(1, 4)]
+        for i, at in parts:
+            copy = pltpu.make_async_copy(ins[i].at[at, :], outs[i].at[at, :], sem.at[len(copies)])
             copy.start()
             copies.append(copy)
         for i in range(4):
@@ -518,7 +536,7 @@
         in_specs=[pl.BlockSpec(memory_space=pltpu.VMEM)] * 5,
         out_specs=[pl.BlockSpec(memory_space=pl.ANY)] * 4
         + [pl.BlockSpec(memory_space=pltpu.SMEM)] * 2,
-        scratch_shapes=[pltpu.SemaphoreType.DMA((4,))],
+        scratch_shapes=[pltpu.SemaphoreType.DMA((11,))],
     )(*[pltpu.with_memory_space_constraint(x, pltpu.VMEM) for x in (v1, v2, v3, v4, stats)])
 
 
@@ -540,6 +558,8 @@
         vmem(2 * packed, LANES), vmem(2 * packed, LANES),
         vmem(2 * packed, LANES), vmem(2 * packed, LANES),
         vmem(4 * HALO, LANES), vmem(4 * HALO, LANES, dtype=jnp.int32),
+        vmem(blocks * ROW_CHUNK, 512, dtype=BF16), vmem(blocks * ROW_CHUNK, 256, dtype=BF16),
+        vmem(blocks * ROW_CHUNK, 256), vmem(blocks * ROW_CHUNK, 256),
         vmem(blocks * ROW_CHUNK, 512, dtype=BF16), vmem(blocks * ROW_CHUNK, 256, dtype=BF16),
         vmem(blocks * ROW_CHUNK, 256), vmem(blocks * ROW_CHUNK, 256),
         vmem(rows + 2 * HALO, 256, dtype=BF16), vmem(rows + 2 * HALO, LANES, dtype=BF16),

time: 30.6 us -> 27.8 us (0.908)
  Pallas kernels: 29.7 us -> 26.9 us
    pallas_call x1, Pallas kernels: 28.1 us -> 25.2 us  [per_device(): pl.pallas_call(kernel, out_shape=out_shape, in_specs=[pl.BlockSpec(memory...]
where the time goes in v2:
time: 27.8 us; the launch traced here: 27.5 us
  Pallas kernels  26.9 us (97%)
  between operations  0.64 us (2%)
    pallas_call x1, Pallas kernels, per_device(): pl.pallas_call(kernel, out_shape=out_shape, in_specs=[pl.BlockSpec(memory...  25.2 us
    pallas_call x1, Pallas kernels, copy_out(): pl.pallas_call(body, out_shape=shapes, in_specs=[pl.BlockSpec(memory_spac...  1.69 us

profile of v2, /device:TPU:1, one launch (start us, length us, event | category | flops | bytes accessed | tf_op | source)
XLA Modules:
  0.0 27.5 jit_solution(6934499909254807220)
XLA Ops:
  0.6 25.2 %shard_map.73 = (f32[256,1024]{1,0:T(8,128)S(1)}, f32[128,512]{1,0:T(8,128)S(1)}, f32[64,256]{1,0:T(8,128)S(1)}, f32[32,128]{1,0:T(8,128)S(1)}, f32[8,128]{1,0:T(8,128)S(1)}) custom-call(f32[512,2048]{1,0:T(8,128)} %field_hbm.1, s32[64,512]{1,0:T(8,128)} %bitcast.1), custom_call_target="tpu_custom_call" | custom-call | tf_op jit(solution)/shard_map/pallas_call | solution.py:587
  25.8 1.7 %shard_map.74 = (f32[256,1024]{1,0:T(8,128)}, f32[128,512]{1,0:T(8,128)}, f32[64,256]{1,0:T(8,128)}, f32[32,128]{1,0:T(8,128)}, f32[4]{0:T(128)}, /*index=5*/f32[4]{0:T(128)}) custom-call(f32[256,1024]{1,0:T(8,128)S(1)} %get-tuple-element.11.refs_0_, f32[128,512]{1,0:T(8,128)S(1)} %get-tuple-element.12.refs_1_, f32[64,256]{1,0:T(8,128)S(1)} %get-tuple-element.13.refs_2_, ...), custom_call_target="tpu_custom_call" | custom-call | tf_op jit(solution)/shard_map/pallas_call | solution.py:533

commit v3 on v2

--- a/solution.py
+++ b/solution.py
@@ -113,6 +113,7 @@
     hn, hd, cosb, p1, d1, p2, d2, p3, d3,
     sx, sxe, rx, rxe, band, edge, msg_a, msg_b, slot_a, slot_b,
     load_sem, send_sem, recv_sem, a_send, a_recv, b_send, b_recv,
+    beside_sem, far_sem,
 ):
     n_rows, n_cols = lax.axis_size("rows"), lax.axis_size("cols")
     my_row, my_col = lax.axis_index("rows"), lax.axis_index("cols")
@@ -122,9 +123,15 @@
     left, right = lax.rem(my_col + n_cols - 1, n_cols), lax.rem(my_col + 1, n_cols)
 
     barrier = pltpu.get_barrier_semaphore()
+    half_rows = n_rows // 2
+    half_start = my_row // half_rows * half_rows
+    far_row = lax.rem(my_row + half_rows, n_rows)
     peers = [(my_row, lax.rem(my_col + s, n_cols)) for s in range(1, n_cols)]
-    peers += [(lax.rem(my_row + s, n_rows), my_col) for s in range(1, n_rows)]
-    peers += [(up, left), (up, right), (down, left), (down, right)]
+    peers += [
+        (half_start + lax.rem(my_row - half_start + s, half_rows), my_col)
+        for s in range(1, half_rows)
+    ]
+    peers += [(far_row, my_col), (up, my_col), (down, my_col)]
     for peer in peers:
         pl.semaphore_signal(barrier, inc=1, device_id=peer, device_id_type=MESH)
 
@@ -216,6 +223,42 @@
     send(fld.at[bottom, :], fhal.at[0:HALO, :], down, my_col)
     send(wrd.at[top, :], whal.at[HALO : 2 * HALO, :], up, my_col)
     send(wrd.at[bottom, :], whal.at[0:HALO, :], down, my_col)
+    for column in (left, right):
+        pl.semaphore_signal(
+            beside_sem, inc=1, device_id=(my_row, column), device_id_type=MESH
+        )
+    pl.semaphore_signal(far_sem, inc=1, device_id=(far_row, my_col), device_id_type=MESH)
+
+    for c in order[2:]:
+        load_chunk[c].wait()
+
+    sets = ((s_num, s_den, r_num, r_den), (s_num2, s_den2, r_num2, r_den2))
+
+    def own_mask(at, which):
+        def field_tile(tile):
+            return fld[pl.ds(at, ROW_CHUNK), tile * LANES : (tile + 1) * LANES]
+
+        mask_step(
+            field_tile, wrd[pl.ds(at, ROW_CHUNK), :], ROW_CHUNK, *sets[which][0:2], tiles
+        )
+
+    def own_across(at, which):
+        def store(which, tile, value):
+            ref = (hn, hd)[which]
+            ref[tile, pl.ds(PAD + at, ROW_CHUNK), :] = value
+
+        across_step(ROW_CHUNK, *sets[which], band, tiles, store)
+
+    def own_chunks(first, last):
+        own_mask(first * ROW_CHUNK, first % 2)
+        for c in range(first, last):
+            if c + 1 < last:
+                own_mask((c + 1) * ROW_CHUNK, (c + 1) % 2)
+            own_across(c * ROW_CHUNK, c % 2)
+
+    own_chunks(0, chunks // 2)
+
+    pl.semaphore_wait(beside_sem, 2)
     send(fld.at[bottom, last_tile], cornf.at[0 * HALO : 1 * HALO, :], down, right)
     send(fld.at[bottom, 0:LANES], cornf.at[1 * HALO : 2 * HALO, :], down, left)
     send(fld.at[top, last_tile], cornf.at[2 * HALO : 3 * HALO, :], up, right)
@@ -225,31 +268,7 @@
     send(wrd.at[top, :], cornw.at[2 * HALO : 3 * HALO, :], up, right)
     send(wrd.at[top, :], cornw.at[3 * HALO : 4 * HALO, :], up, left)
 
-    for c in order[2:]:
-        load_chunk[c].wait()
-
-    sets = ((s_num, s_den, r_num, r_den), (s_num2, s_den2, r_num2, r_den2))
-
-    def own_mask(at, which):
-        def field_tile(tile):
-            return fld[pl.ds(at, ROW_CHUNK), tile * LANES : (tile + 1) * LANES]
-
-        mask_step(
-            field_tile, wrd[pl.ds(at, ROW_CHUNK), :], ROW_CHUNK, *sets[which][0:2], tiles
-        )
-
-    def own_across(at, which):
-        def store(which, tile, value):
-            ref = (hn, hd)[which]
-            ref[tile, pl.ds(PAD + at, ROW_CHUNK), :] = value
-
-        across_step(ROW_CHUNK, *sets[which], band, tiles, store)
-
-    own_mask(0, 0)
-    for c in range(chunks):
-        if c + 1 < chunks:
-            own_mask((c + 1) * ROW_CHUNK, (c + 1) % 2)
-        own_across(c * ROW_CHUNK, c % 2)
+    own_chunks(chunks // 2, chunks)
 
     inside_top, inside_bottom = my_row > 0, my_row < n_rows - 1
     out_rows, out_tiles = rows // 2, tiles // 2
@@ -354,53 +373,22 @@
     merge_edge(0, PAD, rows)
     sums_one = level_one_inner((0, out_tiles - 1, out_tiles), sums_one)
 
-    for copy in sends[2:]:
-        copy.wait()
-
-    def halo_store(which, tile, value):
-        ref = (hn, hd)[which]
-        ref[tile, PAD - HALO : PAD, :] = value[0:HALO, :]
-        ref[tile, PAD + rows : PAD + rows + HALO, :] = value[HALO : 2 * HALO, :]
-
-    first_across(
-        lambda tile: fhal[:, tile * LANES : (tile + 1) * LANES], whal[...], 2 * HALO,
-        s_num, s_den, r_num, r_den, band, tiles, halo_store,
-    )
-    lane16 = lane_iota(HALO)
-    for side in range(2):
-        l_at = slice(2 * side * HALO, (2 * side + 1) * HALO)
-        r_at = slice((2 * side + 1) * HALO, (2 * side + 2) * HALO)
-        is_right, is_left = lane16 < HALO, lane16 >= LANES - HALO
-        value = jnp.where(is_right, cornf[r_at, :], jnp.where(is_left, cornf[l_at, :], 0.0))
-        land_r = jnp.where(land_of(cornw[r_at, :], 0), 1.0, 0.0)
-        land_l = jnp.where(land_of(cornw[l_at, :], tiles - 1), 1.0, 0.0)
-        land = jnp.where(is_right, land_r, jnp.where(is_left, land_l, 0.0))
-        edge_store(rows + side * HALO, HALO, value, land)
-    edge_dot(rows, 2 * HALO)
-    merge_edge(rows, PAD - HALO, HALO)
-    merge_edge(rows + HALO, PAD + rows, HALO)
-    for i0 in (0, out_rows - 8):
-        sums_one = level_one_own(i0, range(out_tiles + 1), sums_one)
-    level_one_beyond(-8, inside_top)
-    level_one_beyond(out_rows, inside_bottom)
-    all_sums = [sums_one]
+    def row_groups(ref):
+        return [(i0, i0 + 8) for i0 in range(0, ref.shape[0], 16)]
 
     def next_level(pin, din, pout, dout, vout):
         out_rows, out_cols = vout.shape
         blocks = out_cols // LANES
         last_level = pout is None
-        groups = [(i0, i0 + 8) for i0 in range(0, out_rows, 16)]
-        parts = [groups[i : i + 4] for i in range(0, len(groups), 4)]
-        if not last_level:
-            parts.append([(-8, out_rows)])
+        next_free = [0, 0]
         low_half = lane_iota(8) < 64
 
         def down_rows(ref, i0, tile):
             taps = [ref[tile, pl.ds(PAD + 2 * i0 - 1 + a, 8, stride=2), :] for a in range(4)]
             return 0.125 * (taps[0] + taps[3]) + 0.375 * (taps[1] + taps[2])
 
-        sums, base, base_e = zero_sums, 0, 0
-        for part in parts:
+        def run(part, sums):
+            base, base_e = next_free
             count = 16 * len(part)
             for g, pair in enumerate(part):
                 for which, ref in ((0, pin), (1, din)):
@@ -454,13 +442,54 @@
                     if tile < blocks:
                         vout[i0 : i0 + 8, tile * LANES : (tile + 1) * LANES] = value
                         sums = gather_sums(sums, value, product, both[1])
-            base += total
-            base_e += 2 * count
-        return sums
-
-    all_sums.append(next_level(p1, d1, p2, d2, v2))
-    all_sums.append(next_level(p2, d2, p3, d3, v3))
-    all_sums.append(next_level(p3, d3, None, None, v4))
+            next_free[0], next_free[1] = base + total, base_e + 2 * count
+            return sums
+
+        return run
+
+    two = next_level(p1, d1, p2, d2, v2)
+    groups_two = row_groups(v2)
+    middle = groups_two[1:-1]
+    sums_two = zero_sums
+    for i in range(0, len(middle), 3):
+        sums_two = two(middle[i : i + 3], sums_two)
+
+    for copy in sends[2:6]:
+        copy.wait()
+
+    def halo_store(which, tile, value):
+        ref = (hn, hd)[which]
+        ref[tile, PAD - HALO : PAD, :] = value[0:HALO, :]
+        ref[tile, PAD + rows : PAD + rows + HALO, :] = value[HALO : 2 * HALO, :]
+
+    first_across(
+        lambda tile: fhal[:, tile * LANES : (tile + 1) * LANES], whal[...], 2 * HALO,
+        s_num, s_den, r_num, r_den, band, tiles, halo_store,
+    )
+    for copy in sends[6:]:
+        copy.wait()
+    lane16 = lane_iota(HALO)
+    for side in range(2):
+        l_at = slice(2 * side * HALO, (2 * side + 1) * HALO)
+        r_at = slice((2 * side + 1) * HALO, (2 * side + 2) * HALO)
+        is_right, is_left = lane16 < HALO, lane16 >= LANES - HALO
+        value = jnp.where(is_right, cornf[r_at, :], jnp.where(is_left, cornf[l_at, :], 0.0))
+        land_r = jnp.where(land_of(cornw[r_at, :], 0), 1.0, 0.0)
+        land_l = jnp.where(land_of(cornw[l_at, :], tiles - 1), 1.0, 0.0)
+        land = jnp.where(is_right, land_r, jnp.where(is_left, land_l, 0.0))
+        edge_store(rows + side * HALO, HALO, value, land)
+    edge_dot(rows, 2 * HALO)
+    merge_edge(rows, PAD - HALO, HALO)
+    merge_edge(rows + HALO, PAD + rows, HALO)
+    for i0 in (0, out_rows - 8):
+        sums_one = level_one_own(i0, range(out_tiles + 1), sums_one)
+    level_one_beyond(-8, inside_top)
+    level_one_beyond(out_rows, inside_bottom)
+    sums_two = two([groups_two[0], groups_two[-1], (-8, v2.shape[0])], sums_two)
+    groups_three = row_groups(v3) + [(-8, v3.shape[0])]
+    sums_three = next_level(p2, d2, p3, d3, v3)(groups_three, zero_sums)
+    sums_four = next_level(p3, d3, None, None, v4)(row_groups(v4), zero_sums)
+    all_sums = [sums_one, sums_two, sums_three, sums_four]
 
     lane = lane_iota(1)
     message = jnp.zeros((1, LANES), F32)
@@ -499,6 +528,7 @@
             copy.wait_send()
         return jnp.where(lane < 8, added, largest)
 
+    pl.semaphore_wait(far_sem, 1)
     message = exchange(
         message, msg_b, slot_b, b_send, b_recv, my_row, n_rows, lambda peer: (peer, my_col)
     )
@@ -513,7 +543,8 @@
 
 def copy_out(v1, v2, v3, v4, stats):
     def body(*refs):
-        ins, outs, means, maxima, sem = refs[:5], refs[5:9], refs[9], refs[10], refs[11]
+        ins, outs, small_outs = refs[:5], refs[5:9], refs[9:11]
+        small, sem = refs[11:13], refs[13]
         copies = []
         steps = ins[0].shape[0] // 8
         parts = [(0, pl.ds(k * steps, steps)) for k in range(8)]
@@ -522,9 +553,12 @@
             copy = pltpu.make_async_copy(ins[i].at[at, :], outs[i].at[at, :], sem.at[len(copies)])
             copy.start()
             copies.append(copy)
-        for i in range(4):
-            means[i] = ins[4][0, i]
-            maxima[i] = ins[4][1, i]
+        for which in range(2):
+            for i in range(4):
+                small[which][i] = ins[4][which, i]
+            copy = pltpu.make_async_copy(small[which], small_outs[which], sem.at[len(copies)])
+            copy.start()
+            copies.append(copy)
         for copy in copies:
             copy.wait()
 
@@ -534,9 +568,8 @@
         body,
         out_shape=shapes,
         in_specs=[pl.BlockSpec(memory_space=pltpu.VMEM)] * 5,
-        out_specs=[pl.BlockSpec(memory_space=pl.ANY)] * 4
-        + [pl.BlockSpec(memory_space=pltpu.SMEM)] * 2,
-        scratch_shapes=[pltpu.SemaphoreType.DMA((11,))],
+        out_specs=[pl.BlockSpec(memory_space=pl.ANY)] * 6,
+        scratch_shapes=[pltpu.SMEM((4,), F32)] * 2 + [pltpu.SemaphoreType.DMA((13,))],
     )(*[pltpu.with_memory_space_constraint(x, pltpu.VMEM) for x in (v1, v2, v3, v4, stats)])
 
 
@@ -581,6 +614,7 @@
         pltpu.SemaphoreType.DMA((14,)), pltpu.SemaphoreType.DMA((14,)),
         pltpu.SemaphoreType.DMA((n_cols,)), pltpu.SemaphoreType.DMA((n_cols,)),
         pltpu.SemaphoreType.DMA((n_rows,)), pltpu.SemaphoreType.DMA((n_rows,)),
+        pltpu.SemaphoreType.REGULAR, pltpu.SemaphoreType.REGULAR,
     ]
     out_shape = [pltpu.VMEM(level[l], F32) for l in range(1, 5)]
     out_shape.append(pltpu.VMEM((8, LANES), F32))

time: 27.8 us -> 26.8 us (0.964)
  Pallas kernels: 26.9 us -> 25.9 us
    pallas_call x1, Pallas kernels: 1.69 us -> 1.2 us  [copy_out(): pl.pallas_call(body, out_shape=shapes, in_specs=[pl.BlockSpec(memory_spac...]
    pallas_call x1, Pallas kernels: 25.2 us -> 24.7 us  [per_device(): pl.pallas_call(kernel, out_shape=out_shape, in_specs=[pl.BlockSpec(memory...]
where the time goes in v3:
time: 26.8 us; the launch traced here: 26.6 us
  Pallas kernels  25.9 us (97%)
  between operations  0.64 us (2%)
    pallas_call x1, Pallas kernels, per_device(): pl.pallas_call(kernel, out_shape=out_shape, in_specs=[pl.BlockSpec(memory...  24.7 us
    pallas_call x1, Pallas kernels, copy_out(): pl.pallas_call(body, out_shape=shapes, in_specs=[pl.BlockSpec(memory_spac...  1.2 us

profile of v3, /device:TPU:1, one launch (start us, length us, event | category | flops | bytes accessed | tf_op | source)
XLA Modules:
  0.0 26.6 jit_solution(1762837778830450205)
XLA Ops:
  0.6 24.7 %shard_map.73 = (f32[256,1024]{1,0:T(8,128)S(1)}, f32[128,512]{1,0:T(8,128)S(1)}, f32[64,256]{1,0:T(8,128)S(1)}, f32[32,128]{1,0:T(8,128)S(1)}, f32[8,128]{1,0:T(8,128)S(1)}) custom-call(f32[512,2048]{1,0:T(8,128)} %field_hbm.1, s32[64,512]{1,0:T(8,128)} %bitcast.1), custom_call_target="tpu_custom_call" | custom-call | tf_op jit(solution)/shard_map/pallas_call | solution.py:621
  25.4 1.2 %shard_map.74 = (f32[256,1024]{1,0:T(8,128)}, f32[128,512]{1,0:T(8,128)}, f32[64,256]{1,0:T(8,128)}, f32[32,128]{1,0:T(8,128)}, f32[4]{0:T(128)}, /*index=5*/f32[4]{0:T(128)}) custom-call(f32[256,1024]{1,0:T(8,128)S(1)} %get-tuple-element.11.refs_0_, f32[128,512]{1,0:T(8,128)S(1)} %get-tuple-element.12.refs_1_, f32[64,256]{1,0:T(8,128)S(1)} %get-tuple-element.13.refs_2_, ...), custom_call_target="tpu_custom_call" | custom-call | tf_op jit(solution)/shard_map/pallas_call | solution.py:567

commit v4 on v3

--- a/solution.py
+++ b/solution.py
@@ -126,12 +126,15 @@
     half_rows = n_rows // 2
     half_start = my_row // half_rows * half_rows
     far_row = lax.rem(my_row + half_rows, n_rows)
-    peers = [(my_row, lax.rem(my_col + s, n_cols)) for s in range(1, n_cols)]
+    peers = [(up, my_col), (down, my_col), (far_row, my_col)]
+    peers += [
+        (my_row, lax.rem(my_col + s, n_cols))
+        for s in sorted(range(1, n_cols), key=lambda s: min(s, n_cols - s))
+    ]
     peers += [
         (half_start + lax.rem(my_row - half_start + s, half_rows), my_col)
         for s in range(1, half_rows)
     ]
-    peers += [(far_row, my_col), (up, my_col), (down, my_col)]
     for peer in peers:
         pl.semaphore_signal(barrier, inc=1, device_id=peer, device_id_type=MESH)
 
@@ -256,7 +259,7 @@
                 own_mask((c + 1) * ROW_CHUNK, (c + 1) % 2)
             own_across(c * ROW_CHUNK, c % 2)
 
-    own_chunks(0, chunks // 2)
+    own_chunks(0, 3 * chunks // 4)
 
     pl.semaphore_wait(beside_sem, 2)
     send(fld.at[bottom, last_tile], cornf.at[0 * HALO : 1 * HALO, :], down, right)
@@ -268,7 +271,7 @@
     send(wrd.at[top, :], cornw.at[2 * HALO : 3 * HALO, :], up, right)
     send(wrd.at[top, :], cornw.at[3 * HALO : 4 * HALO, :], up, left)
 
-    own_chunks(chunks // 2, chunks)
+    own_chunks(3 * chunks // 4, chunks)
 
     inside_top, inside_bottom = my_row > 0, my_row < n_rows - 1
     out_rows, out_tiles = rows // 2, tiles // 2
@@ -373,14 +376,22 @@
     merge_edge(0, PAD, rows)
     sums_one = level_one_inner((0, out_tiles - 1, out_tiles), sums_one)
 
-    def row_groups(ref):
-        return [(i0, i0 + 8) for i0 in range(0, ref.shape[0], 16)]
+    def inner_groups(ref):
+        return [(i0, i0 + 8) for i0 in range(8, ref.shape[0] - 8, 16)]
+
+    def outer_groups(ref, beyond):
+        own = [(0, ref.shape[0] - 8)]
+        return own + [(-8, ref.shape[0])] if beyond else own
+
+    used = [0, 0]
 
     def next_level(pin, din, pout, dout, vout):
         out_rows, out_cols = vout.shape
         blocks = out_cols // LANES
         last_level = pout is None
-        next_free = [0, 0]
+        next_free = list(used)
+        used[0] += 2 * blocks * (out_rows + HALO)
+        used[1] += 2 * (out_rows + HALO)
         low_half = lane_iota(8) < 64
 
         def down_rows(ref, i0, tile):
@@ -448,11 +459,12 @@
         return run
 
     two = next_level(p1, d1, p2, d2, v2)
-    groups_two = row_groups(v2)
-    middle = groups_two[1:-1]
-    sums_two = zero_sums
-    for i in range(0, len(middle), 3):
-        sums_two = two(middle[i : i + 3], sums_two)
+    three = next_level(p2, d2, p3, d3, v3)
+    four = next_level(p3, d3, None, None, v4)
+    sums_two, sums_three, sums_four = zero_sums, zero_sums, zero_sums
+    groups = inner_groups(v2)
+    for i in range(0, len(groups), 4):
+        sums_two = two(groups[i : i + 4], sums_two)
 
     for copy in sends[2:6]:
         copy.wait()
@@ -485,10 +497,9 @@
         sums_one = level_one_own(i0, range(out_tiles + 1), sums_one)
     level_one_beyond(-8, inside_top)
     level_one_beyond(out_rows, inside_bottom)
-    sums_two = two([groups_two[0], groups_two[-1], (-8, v2.shape[0])], sums_two)
-    groups_three = row_groups(v3) + [(-8, v3.shape[0])]
-    sums_three = next_level(p2, d2, p3, d3, v3)(groups_three, zero_sums)
-    sums_four = next_level(p3, d3, None, None, v4)(row_groups(v4), zero_sums)
+    sums_two = two(outer_groups(v2, True), sums_two)
+    sums_three = three(inner_groups(v3) + outer_groups(v3, True), sums_three)
+    sums_four = four(inner_groups(v4) + outer_groups(v4, False), sums_four)
     all_sums = [sums_one, sums_two, sums_three, sums_four]
 
     lane = lane_iota(1)
@@ -500,6 +511,8 @@
     for level, sums in enumerate(all_sums):
         for place, (part, op) in enumerate(zip(sums, (jnp.sum, jnp.sum, jnp.max))):
             message = jnp.where(lane == 4 * place + level, whole(part, op), message)
+
+    sent = []
 
     def exchange(message, buffer, slots, send_sems, recv_sems, index, count, device):
         buffer[...] = message
@@ -524,8 +537,7 @@
         added, largest = slots[0], slots[0]
         for i in range(1, count):
             added, largest = added + slots[i], jnp.maximum(largest, slots[i])
-        for copy in copies:
-            copy.wait_send()
+        sent.extend(copies)
         return jnp.where(lane < 8, added, largest)
 
     pl.semaphore_wait(far_sem, 1)
@@ -539,6 +551,8 @@
     covers = pltpu.roll(wide, LANES - 4, 1)
     maxima = pltpu.roll(wide, LANES - 8, 1)
     stats[...] = jnp.where(sub == 0, wide / (covers + EPS), maxima)
+    for copy in sent:
+        copy.wait_send()
 
 
 def copy_out(v1, v2, v3, v4, stats):
@@ -602,11 +616,11 @@
     ]
     for l in range(1, 4):
         scratch += [vmem(level[l][1] // LANES + 1, level[l][0] + 2 * PAD, LANES)] * 2
-    count = level[2][0] + HALO
-    inner_blocks = level[2][1] // LANES
+    count = sum(level[l][0] + HALO for l in range(2, 5))
+    stacked = sum(2 * (level[l][1] // LANES) * (level[l][0] + HALO) for l in range(2, 5))
     scratch += [
-        vmem(2 * inner_blocks * count, 512, dtype=BF16), vmem(2 * count, 256, dtype=BF16),
-        vmem(2 * inner_blocks * count, 256), vmem(2 * count, 256),
+        vmem(stacked, 512, dtype=BF16), vmem(2 * count, 256, dtype=BF16),
+        vmem(stacked, 256), vmem(2 * count, 256),
         vmem(512, 256, dtype=BF16), vmem(256, 256, dtype=BF16),
         vmem(1, LANES), vmem(1, LANES),
         vmem(n_cols, 1, LANES), vmem(n_rows, 1, LANES),

time: 26.8 us -> 26.9 us (level)
  no operation moved by 1% of the time
where the time goes in v4:
time: 26.9 us; the launch traced here: 26.6 us
  Pallas kernels  26 us (97%)
  between operations  0.64 us (2%)
    pallas_call x1, Pallas kernels, per_device(): pl.pallas_call(kernel, out_shape=out_shape, in_specs=[pl.BlockSpec(memory...  24.8 us
    pallas_call x1, Pallas kernels, copy_out(): pl.pallas_call(body, out_shape=shapes, in_specs=[pl.BlockSpec(memory_spac...  1.2 us

profile of v4, /device:TPU:1, one launch (start us, length us, event | category | flops | bytes accessed | tf_op | source)
XLA Modules:
  0.0 26.6 jit_solution(16866862975028653512)
XLA Ops:
  0.6 24.8 %shard_map.73 = (f32[256,1024]{1,0:T(8,128)S(1)}, f32[128,512]{1,0:T(8,128)S(1)}, f32[64,256]{1,0:T(8,128)S(1)}, f32[32,128]{1,0:T(8,128)S(1)}, f32[8,128]{1,0:T(8,128)S(1)}) custom-call(f32[512,2048]{1,0:T(8,128)} %field_hbm.1, s32[64,512]{1,0:T(8,128)} %bitcast.1), custom_call_target="tpu_custom_call" | custom-call | tf_op jit(solution)/shard_map/pallas_call | solution.py:635
  25.4 1.2 %shard_map.74 = (f32[256,1024]{1,0:T(8,128)}, f32[128,512]{1,0:T(8,128)}, f32[64,256]{1,0:T(8,128)}, f32[32,128]{1,0:T(8,128)}, f32[4]{0:T(128)}, /*index=5*/f32[4]{0:T(128)}) custom-call(f32[256,1024]{1,0:T(8,128)S(1)} %get-tuple-element.11.refs_0_, f32[128,512]{1,0:T(8,128)S(1)} %get-tuple-element.12.refs_1_, f32[64,256]{1,0:T(8,128)S(1)} %get-tuple-element.13.refs_2_, ...), custom_call_target="tpu_custom_call" | custom-call | tf_op jit(solution)/shard_map/pallas_call | solution.py:581
